TPU v7x, 32 devices: a whole 2x2x4 slice. The times are simulated.
32 devices in a mesh: dp: 4 (over z), blk: 2 (over y), head: 4 (over x, core).
Axes of the slice: x: 2, y: 2, z: 4, core: 2. Of those that a mesh axis runs over, the one named last changes fastest.
Arguments:
- queries: bfloat16 [4, 1024, 1024], P('dp', ('blk', 'head')), may hold values from -40 to 40
- keys_values: bfloat16 [4, 1024, 512], P('dp', ('blk', 'head')), may hold values from -40 to 40
- out_weight: bfloat16 [1024, 2048], P('head'), may hold values from -0.125 to 0.125
- cotangent: bfloat16 [4, 1024, 2048], P('dp', ('blk', 'head')), may hold values from -6 to 6
- passage_lengths: int32 [4, 32], P('dp'), may hold values from 1 to 64, 992 in all within a row
- causal_flags: int32 [4, 32], P('dp'), may hold values from 0 to 1
Outputs:
- attn: bfloat16 [4, 1024, 1024], P('dp', 'blk', 'head')
- grad_queries: bfloat16 [4, 1024, 1024], P('dp', 'blk', 'head')
- grad_keys_values: bfloat16 [4, 1024, 512], P('dp', 'blk', 'head')
- grad_out_weight: bfloat16 [1024, 2048], P('head')
Inputs may be any that keep to these rules, and one draw needn't show every extreme that they name: `passage_lengths`: each row sums to 992; its largest entry is 64.
All inputs are finite; a program needn't handle non-finite values.
Results may differ from a plain program's by a relative error of at most 0.019.
Values may be sent and summed in bfloat16 or wider, within the bound.
A program may use at most 128 MiB of HBM per device.

v0:
```python
import jax
import jax.numpy as jnp
from jax import lax
from jax.sharding import PartitionSpec as P

neg_fill = -1e30


def passed_along(value, axis, steps):
    count = lax.axis_size(axis)
    pairs = [(source, (source + steps) % count) for source in range(count)]
    return lax.ppermute(value, axis, pairs)


def describe(lengths, causal, positions, prefix):
    starts = prefix + jnp.cumsum(lengths) - lengths
    segment_id = jnp.sum((starts[None, :] <= positions[:, None]).astype(jnp.int32), axis=1)
    labels = jnp.arange(1, lengths.shape[0] + 1, dtype=jnp.int32)
    flag_of = jnp.sum(jnp.where(segment_id[:, None] == labels[None, :], causal[None, :], 0), axis=1)
    flag_of = flag_of + (segment_id == 0).astype(jnp.int32)
    return (segment_id, flag_of)


def permitted(query_info, key_info, query_pos, key_pos):
    query_seg, query_flag = query_info
    key_seg, key_flag = key_info
    same_list = query_seg[:, None] == key_seg[None, :]
    visible = same_list | (key_seg[None, :] == 0)
    ordered = (key_pos[None, :] <= query_pos[:, None]) | (query_flag[:, None] == 0) & same_list
    return visible & ordered


def on_device(queries, keys_values, out_weight, cotangent, passage_lengths, causal_flags):
    q_rows, kv_rows = (
        lax.all_to_all(queries[0], "head", split_axis=1, concat_axis=0, tiled=True),
        lax.all_to_all(keys_values[0], "head", split_axis=1, concat_axis=0, tiled=True),
    )
    local_rows = q_rows.shape[0]
    cycle_size = lax.axis_size("blk")
    own_index = lax.axis_index("blk")
    seq_total = local_rows * cycle_size
    prefix = seq_total // 32
    head_dim = kv_rows.shape[1] // 2
    head_count = q_rows.shape[1] // head_dim
    flat_rows = local_rows * head_count
    scale = head_dim ** (-0.5)
    lengths = passage_lengths[0]
    causal = causal_flags[0]
    query_pos = own_index * local_rows + jnp.arange(local_rows, dtype=jnp.int32)
    query_info = describe(lengths, causal, query_pos, prefix)
    q_flat = q_rows.reshape(flat_rows, head_dim)

    def allowed_for(key_start, span_rows, floor_pos, live):
        key_pos = key_start + jnp.arange(span_rows, dtype=jnp.int32)
        allowed = permitted(
            query_info, describe(lengths, causal, key_pos, prefix), query_pos, key_pos
        )
        allowed = allowed & (key_pos >= floor_pos)[None, :] & live
        expanded = jnp.broadcast_to(
            allowed[:, None, :], (local_rows, head_count, span_rows)
        ).reshape(flat_rows, span_rows)
        return (allowed, expanded)

    def score_block(key_block):
        return (
            lax.dot_general(
                q_flat,
                key_block[:, :head_dim],
                (((1,), (1,)), ((), ())),
                preferred_element_type=jnp.float32,
            )
            * scale
        )

    def visit(state, key_block, key_start, floor_pos, live):
        allowed, expanded = allowed_for(key_start, key_block.shape[0], floor_pos, live)

        def visit_compute(inner):
            running_max, totals = inner
            scores = score_block(key_block)
            block_max = jnp.max(jnp.where(expanded, scores, neg_fill), axis=1)
            new_best = jnp.maximum(running_max, block_max)
            factor = jnp.exp(running_max - new_best)
            weights = jnp.where(expanded, jnp.exp(scores - new_best[:, None]), 0.0)
            totals = totals * factor + jnp.sum(weights, axis=1)
            return (new_best, totals)

        def visit_keep(inner):
            return inner

        return lax.cond(jnp.any(allowed), visit_compute, visit_keep, state)

    state_start = (
        jnp.full((flat_rows,), neg_fill, jnp.float32),
        jnp.zeros((flat_rows,), jnp.float32),
    )
    always = jnp.array(True)
    initial = (jnp.zeros((seq_total, 2 * head_dim), jnp.bfloat16),) + state_start
    shard_rows = lax.all_gather(kv_rows, "blk", axis=0, tiled=True)

    def one_block(index, inner):
        key_block = lax.dynamic_slice_in_dim(shard_rows, index * local_rows, local_rows, 0)
        return visit(inner, key_block, index * local_rows, 0, always)

    inner = lax.fori_loop(0, shard_rows.shape[0] // local_rows, one_block, tuple(initial[1:]))
    stored, running_max, totals = (shard_rows,) + tuple(inner)
    log_norm = running_max + jnp.log(totals)

    def stored_rows(key_start, span_rows):
        return lax.dynamic_slice_in_dim(stored, key_start, span_rows, 0)

    def add_values(accum, key_block, key_start, floor_pos, live):
        allowed, expanded = allowed_for(key_start, key_block.shape[0], floor_pos, live)

        def add_compute(acc_in):
            scores = score_block(key_block)
            probs = jnp.where(expanded, jnp.exp(scores - log_norm[:, None]), 0.0)
            return acc_in + jnp.dot(
                probs.astype(jnp.bfloat16),
                key_block[:, head_dim:],
                preferred_element_type=jnp.float32,
            )

        def add_keep(acc_in):
            return acc_in

        return lax.cond(jnp.any(allowed), add_compute, add_keep, accum)

    accum = jnp.zeros((flat_rows, head_dim), jnp.float32)

    def value_turn(index, acc_in):
        return add_values(
            acc_in, stored_rows(index * local_rows, local_rows), index * local_rows, 0, always
        )

    accum = lax.fori_loop(0, cycle_size, value_turn, accum)
    attn = accum.reshape(local_rows, head_count * head_dim).astype(jnp.bfloat16)
    project_shard_rows = lax.all_gather(cotangent[0], "head", axis=0, tiled=True)
    product = lax.dot_general(
        project_shard_rows, out_weight, (((1,), (1,)), ((), ())), preferred_element_type=jnp.float32
    )
    grads = product
    weight_acc = lax.dot_general(
        attn, project_shard_rows, (((0,), (0,)), ((), ())), preferred_element_type=jnp.float32
    )
    grads, weight_acc = (grads, weight_acc)
    attention_gradient = grads.astype(jnp.bfloat16)
    d_flat = attention_gradient.reshape(flat_rows, head_dim)
    row_dot = jnp.sum(
        (attention_gradient.astype(jnp.float32) * attn.astype(jnp.float32)).reshape(
            flat_rows, head_dim
        ),
        axis=1,
    )
    shares = lax.psum_scatter(
        weight_acc.astype(jnp.bfloat16), "blk", scatter_dimension=1, tiled=True
    ).astype(jnp.float32)
    shares = lax.psum(shares.astype(jnp.bfloat16), "dp")
    grad_weight = lax.all_gather(shares, "blk", axis=1, tiled=True)

    def contribute(grad_q, key_block, key_start, floor_pos, live):
        span_rows = key_block.shape[0]
        allowed, expanded = allowed_for(key_start, span_rows, floor_pos, live)

        def contribute_compute(grad_in):
            scores = score_block(key_block)
            probs = jnp.where(expanded, jnp.exp(scores - log_norm[:, None]), 0.0)
            dprob = lax.dot_general(
                d_flat,
                key_block[:, head_dim:],
                (((1,), (1,)), ((), ())),
                preferred_element_type=jnp.float32,
            )
            dscore = (probs * (dprob - row_dot[:, None])).astype(jnp.bfloat16)
            grad_out = grad_in + scale * jnp.dot(
                dscore, key_block[:, :head_dim], preferred_element_type=jnp.float32
            )
            grad_key = scale * lax.dot_general(
                dscore, q_flat, (((0,), (0,)), ((), ())), preferred_element_type=jnp.float32
            )
            grad_value = lax.dot_general(
                probs.astype(jnp.bfloat16),
                d_flat,
                (((0,), (0,)), ((), ())),
                preferred_element_type=jnp.float32,
            )
            return (grad_out, jnp.concatenate([grad_key, grad_value], axis=1))

        def skip(grad_in):
            return (grad_in, jnp.zeros((span_rows, 2 * head_dim), jnp.float32))

        return lax.cond(jnp.any(allowed), contribute_compute, skip, grad_q)

    grad_start = jnp.zeros((flat_rows, head_dim), jnp.float32)

    def turn_single(turn_index, state):
        grad_q, passing = state
        target = (own_index - 1 - turn_index) % cycle_size
        grad_q, piece_grad = contribute(
            grad_q, stored_rows(target * local_rows, local_rows), target * local_rows, 0, always
        )
        passing = passed_along((passing + piece_grad).astype(jnp.bfloat16), "blk", 1).astype(
            jnp.float32
        )
        return (grad_q, passing)

    zero_full = jnp.zeros((local_rows, 2 * head_dim), jnp.float32)
    grad_q, passing = lax.fori_loop(0, cycle_size - 1, turn_single, (grad_start, zero_full))
    grad_q, piece_grad = contribute(
        grad_q, stored_rows(own_index * local_rows, local_rows), own_index * local_rows, 0, always
    )
    key_value_gradient = passing + piece_grad
    grad_queries = grad_q.reshape(local_rows, head_count * head_dim).astype(jnp.bfloat16)
    return (
        attn[None],
        grad_queries[None],
        key_value_gradient.astype(jnp.bfloat16)[None],
        grad_weight,
    )


def solution(mesh):
    return jax.shard_map(
        on_device,
        mesh=mesh,
        in_specs=(
            P("dp", ("blk", "head"), None),
            P("dp", ("blk", "head"), None),
            P("head", None),
            P("dp", ("blk", "head"), None),
            P("dp", None),
            P("dp", None),
        ),
        out_specs=(
            P("dp", "blk", "head"),
            P("dp", "blk", "head"),
            P("dp", "blk", "head"),
            P("head", None),
        ),
        check_vma=False,
    )
```

profile of v0, /device:TPU:0, one launch (start us, length us, event | category | flops | bytes accessed | tf_op | source)
XLA Modules:
  0.0 194.0 jit_solution(648378593899598063)
XLA Ops:
  9.5 4.2 %all-to-all-start = ((bf16[128,4,128]{2,0,1:T(8,128)(2,1)}), bf16[128,4,128]{2,0,1:T(8,128)(2,1)S(1)}, u32[]{:S(2)}, u32[]{:S(2)}) async-start(bf16[128,4,128]{2,0,1:T(8,128)(2,1)} %copy.44), calls=%async_computation | async-start | bytes 262144 | tf_op jit(solution)/shard_map/all_to_all | solution.py:36
  16.2 1.1 all_to_all.30
  18.4 3.4 %all-to-all-start.1 = ((bf16[128,4,256]{2,0,1:T(8,128)(2,1)}), bf16[128,4,256]{2,0,1:T(8,128)(2,1)S(1)}, u32[]{:S(2)}, u32[]{:S(2)}) async-start(bf16[128,4,256]{2,0,1:T(8,128)(2,1)} %copy.45), calls=%async_computation.1 | async-start | bytes 524288 | tf_op jit(solution)/shard_map/all_to_all | solution.py:35
  21.8 6.8 %all_gather.9 = bf16[1024,128]{1,0:T(8,128)(2,1)S(1)} all-gather(bf16[512,128]{1,0:T(8,128)(2,1)S(1)} %bitcast.77), channel_id=1, replica_groups=mesh['dp'=4,'blk'=2,'head'=4] {'blk'}, dimensions={0}, use_global_device_ids=true | all-gather | bytes 393216 | tf_op jit(solution)/shard_map/all_gather | solution.py:99
  28.6 2.4 %all-to-all-done.1 = bf16[128,4,256]{2,0,1:T(8,128)(2,1)S(1)} async-done(((bf16[128,4,256]{2,0,1:T(8,128)(2,1)}), bf16[128,4,256]{2,0,1:T(8,128)(2,1)S(1)}, u32[]{:S(2)}, u32[]{:S(2)}) %all-to-all-start.1) | async-done | bytes 262176 | tf_op jit(solution)/shard_map/all_to_all | solution.py:35
  31.0 1.0 reshape.641
  32.0 18.2 %while.45 = (s32[]{:T(128)}, f32[2048]{0:T(1024)S(1)}, f32[2048]{0:T(1024)S(1)}, s32[512]{0:T(512)S(1)}, s32[1,32]{1,0:T(1,128)S(1)}, /*index=5*/s32[32]{0:T(128...) while((s32[]{:T(128)}, f32[2048]{0:T(1024)S(1)}, ...), condition=%wide.region_10.11_spmd.clone, body=%wide.region_3.10_spmd.clone.sunk | while | flops 145545792 | bytes 16786752 | solution.py:105
  34.5 6.6 %conditional.10 = ((f32[2048]{0:T(1024)S(1)}, f32[2048]{0:T(1024)S(1)})) conditional(s32[]{:T(128)} %convert_element_type.180, (f32[2048]{0:T(1024)S(1)}, f32[2048]{0:T(1024)S(1)}) %tuple.164, (s32[512]{0:T(512)S(1)}, s32[512]{0:T(512)S(1)}, pred[512]{0:T(512)(128)(4,1)S(1)}, s32[512]{0:T(512)S(1)}, s32[512]{0:T(512)S(1)}, ...), branch_computations={%region_6.6_spmd, %region_7.9_spmd} | conditional | flops 143396864 | bytes 16762430 | solution.py:91
  36.9 1.2 copy.39
  38.1 1.9 fusion.4
  40.0 1.1 fusion.7
  43.6 6.6 %conditional.10 = ((f32[2048]{0:T(1024)S(1)}, f32[2048]{0:T(1024)S(1)})) conditional(s32[]{:T(128)} %convert_element_type.180, (f32[2048]{0:T(1024)S(1)}, f32[2048]{0:T(1024)S(1)}) %tuple.164, (s32[512]{0:T(512)S(1)}, s32[512]{0:T(512)S(1)}, pred[512]{0:T(512)(128)(4,1)S(1)}, s32[512]{0:T(512)S(1)}, s32[512]{0:T(512)S(1)}, ...), branch_computations={%region_6.6_spmd, %region_7.9_spmd} | conditional | flops 143396864 | bytes 16762430 | solution.py:91
  46.0 1.2 copy.39
  47.2 1.9 fusion.4
  49.1 1.1 fusion.7
  51.1 18.7 %while.46 = (s32[]{:T(128)}, f32[2048,64]{0,1:T(8,128)}, s32[512]{0:T(512)S(1)}, s32[1,32]{1,0:T(1,128)S(1)}, s32[32]{0:T(128)}, /*index=5*/s32[512]{0:T(512)S(1...) while((s32[]{:T(128)}, f32[2048,64]{0,1:T(8,128)}, ...), condition=%wide.region_16.17_spmd.clone, body=%wide.region_11.16_spmd.clone.sunk | while | flops 276744768 | bytes 8432425 | solution.py:136
  53.6 6.9 %conditional.11 = (f32[2048,64]{0,1:T(8,128)}) conditional(s32[]{:T(128)} %convert_element_type.182, f32[2048,64]{0,1:T(8,128)} %get-tuple-element.1167, (s32[512]{0:T(512)S(1)}, s32[512]{0:T(512)S(1)}, pred[512]{0:T(512)(128)(4,1)S(1)}, s32[512]{0:T(512)S(1)}, s32[512]{0:T(512)S(1)}, /*index=5*/pred[512]{0:T(512)(128)(4,1)S(1)}, ...), branch_computations={%region_14.14_spmd, %region_15.15_spmd} | conditional | flops 274595840 | bytes 8408118 | solution.py:127
  56.0 1.2 copy.41
  57.2 3.3 %convolution_add_fusion = f32[2048,64]{0,1:T(8,128)} fusion(f32[2048,64]{0,1:T(8,128)} %get-tuple-element.793, pred[2048,512]{0,1:T(32,128)(4,1)S(1)} %copy.41, bf16[2048,64]{1,0:T(8,128)(2,1)} %get-tuple-element.803, f32[2048]{0:T(1024)S(1)} %get-tuple-element.804, bf16[1024,128]{1,0:T(8,128)(2,1)S(1)} %get-tuple-element.801, s32[]{:T(128)S(6)} %select_n.57, ...), kind=kOutput, calls=%fused_computation.19 | convolution fusion | flops 272760832 | bytes 2631168 | tf_op jit(solution)/shard_map/while/body/eval_jaxpr/cond/branch_1_fun/dot_general | solution.py:118
  62.9 6.9 %conditional.11 = (f32[2048,64]{0,1:T(8,128)}) conditional(s32[]{:T(128)} %convert_element_type.182, f32[2048,64]{0,1:T(8,128)} %get-tuple-element.1167, (s32[512]{0:T(512)S(1)}, s32[512]{0:T(512)S(1)}, pred[512]{0:T(512)(128)(4,1)S(1)}, s32[512]{0:T(512)S(1)}, s32[512]{0:T(512)S(1)}, /*index=5*/pred[512]{0:T(512)(128)(4,1)S(1)}, ...), branch_computations={%region_14.14_spmd, %region_15.15_spmd} | conditional | flops 274595840 | bytes 8408118 | solution.py:127
  65.3 1.2 copy.41
  66.5 3.3 %convolution_add_fusion = f32[2048,64]{0,1:T(8,128)} fusion(f32[2048,64]{0,1:T(8,128)} %get-tuple-element.793, pred[2048,512]{0,1:T(32,128)(4,1)S(1)} %copy.41, bf16[2048,64]{1,0:T(8,128)(2,1)} %get-tuple-element.803, f32[2048]{0:T(1024)S(1)} %get-tuple-element.804, bf16[1024,128]{1,0:T(8,128)(2,1)S(1)} %get-tuple-element.801, s32[]{:T(128)S(6)} %select_n.57, ...), kind=kOutput, calls=%fused_computation.19 | convolution fusion | flops 272760832 | bytes 2631168 | tf_op jit(solution)/shard_map/while/body/eval_jaxpr/cond/branch_1_fun/dot_general | solution.py:118
  69.8 1.1 convert_element_type.130
  71.6 3.3 %convolution_convert_fusion = bf16[256,2048]{1,0:T(8,128)(2,1)} fusion(bf16[512,256]{1,0:T(8,128)(2,1)S(1)} %convert_element_type.137, bf16[1,512,2048]{2,1,0:T(8,128)(2,1)} %all-gather.6.cloned.1.call-done), kind=kOutput, calls=%fused_computation.96 | convolution fusion | flops 537395200 | bytes 3407872 | tf_op jit(solution)/shard_map/dot_general | solution.py:143
  74.9 21.4 %reduce-scatter.2.cloned.1.call-done = bf16[256,1024]{1,0:T(8,128)(2,1)} async-done(((bf16[256,2048]{1,0:T(8,128)(2,1)}), bf16[256,1024]{1,0:T(8,128)(2,1)}) %reduce-scatter.2.cloned.1.call-update) | async-done | bytes 524304 | tf_op jit(solution)/shard_map/reduce_scatter | solution.py:155
  96.5 40.8 %all-reduce.2.cloned.1.call-done = bf16[256,1024]{1,0:T(8,128)(2,1)} async-done(((bf16[256,1024]{1,0:T(8,128)(2,1)}), bf16[256,1024]{1,0:T(8,128)(2,1)}) %all-reduce.2.cloned.1.call-update) | async-done | bytes 524304 | tf_op jit(solution)/shard_map/psum | solution.py:158
  137.4 1.4 fusion.71
  139.5 3.2 %convert_multiply_fusion = (f32[512,256]{1,0:T(8,128)}, bf16[512,256]{1,0:T(8,128)(2,1)S(1)}) fusion(bf16[512,256]{1,0:T(8,128)(2,1)S(1)} %convert_element_type.137, bf16[256,2048]{1,0:T(8,128)(2,1)S(1)} %copy-done, bf16[1,512,2048]{2,1,0:T(8,128)(2,1)} %all-gather.6.cloned.1.call-done), kind=kOutput, calls=%fused_computation.113 | convolution fusion | flops 537395200 | bytes 4194304 | tf_op jit(solution)/shard_map/dot_general | solution.py:139
  142.9 1.2 reshape.643
  146.4 15.4 %conditional.4 = (f32[2048,64]{0,1:T(8,128)}, bf16[512,128]{0,1:T(8,128)(2,1)S(1)}) conditional(s32[]{:T(128)} %convert_element_type.134, f32[2048,64]{0,1:T(8,128)} %broadcast.644, (s32[512]{0:T(512)S(1)}, s32[512]{0:T(512)S(1)}, pred[512]{0:T(512)(128)(4,1)S(1)}, s32[512]{0:T(512)S(1)}, s32[512,1,512]{2,0,1:T(8,128)S(1)}, ...), branch_computations={%region_21.22_spmd, %region_22.23_spmd} | conditional | flops 680853504 | bytes 30432334 | solution.py:192
  146.4 1.4 fusion.31
  147.8 1.9 broadcast_in_dim.197
  149.7 3.8 %reshape.636 = pred[2048,512]{1,0:T(32,128)(4,1)} reshape(pred[512,4,512]{2,1,0:T(4,128)(4,1)} %broadcast_in_dim.197) | data formatting | bytes 2097152 | tf_op jit(solution)/shard_map/while/body/eval_jaxpr/reshape | solution.py:61
  153.5 2.3 %copy.42 = pred[2048,512]{0,1:T(32,128)(4,1)S(1)} copy(pred[2048,512]{1,0:T(32,128)(4,1)} %reshape.636) | data formatting | bytes 2097152 | tf_op jit(solution)/shard_map/while/body/eval_jaxpr/reshape | solution.py:61
  155.8 1.2 bitcast_select_fusion.2
  159.3 2.4 %fusion.26 = f32[2048,64]{0,1:T(8,128)} fusion(f32[2048,64]{0,1:T(8,128)} %get-tuple-element.816, bf16[2048,512]{0,1:T(8,128)(2,1)S(1)} %fusion.25, bf16[1024,128]{1,0:T(8,128)(2,1)S(1)} %get-tuple-element.824, s32[]{:T(128)S(6)} %select_n.59), kind=kOutput, calls=%fused_computation.34 | convolution fusion | flops 134479872 | bytes 3276804 | tf_op jit(solution)/shard_map/while/body/eval_jaxpr/cond/branch_1_fun/dot_general | solution.py:175
  162.5 1.5 collective-permute-start
  164.6 2.2 %convert_element_type.131 = bf16[1,512,256]{2,1,0:T(8,128)(2,1)} reshape(bf16[2048,64]{1,0:T(8,128)(2,1)} %copy-done.2) | data formatting | bytes 524288 | tf_op jit(solution)/shard_map/convert_element_type | solution.py:137
  166.8 13.6 %conditional.5 = (f32[2048,64]{0,1:T(8,128)}, f32[512,128]{1,0:T(8,128)S(1)}) conditional(s32[]{:T(128)} %convert_element_type.132, f32[2048,64]{0,1:T(8,128)} %get-tuple-element.857, (s32[512]{0:T(512)S(1)}, pred[512]{0:T(512)(128)(4,1)}, s32[512]{0:T(512)S(1)}, s32[512,1,512]{2,0,1:T(8,128)S(1)}, pred[512,1,512]{2,0,1:T(8,128)(4,1)}, ...), branch_computations={%region_23.24_spmd, %region_24.25_spmd} | conditional | flops 680624128 | bytes 31347790 | solution.py:192
  166.8 1.4 fusion.44
  169.2 2.1 %reshape.637 = pred[2048,512]{1,0:T(32,128)(4,1)} reshape(pred[512,4,512]{2,1,0:T(4,128)(4,1)S(1)} %broadcast_in_dim.200) | data formatting | bytes 2097152 | tf_op jit(solution)/shard_map/reshape | solution.py:61
  171.3 2.3 %copy.43 = pred[2048,512]{0,1:T(32,128)(4,1)S(1)} copy(pred[2048,512]{1,0:T(32,128)(4,1)} %reshape.637) | data formatting | bytes 2097152 | tf_op jit(solution)/shard_map/reshape | solution.py:61
  173.6 1.9 bitcast_select_fusion.3
  177.8 2.4 %fusion.39 = f32[2048,64]{0,1:T(8,128)} fusion(f32[2048,64]{0,1:T(8,128)} %get-tuple-element.830, bf16[2048,512]{0,1:T(8,128)(2,1)S(1)} %fusion.38, bf16[1024,128]{1,0:T(8,128)(2,1)S(1)} %get-tuple-element.837, s32[]{:T(128)S(6)} %select_n.61), kind=kOutput, calls=%fused_computation.54 | convolution fusion | flops 134479872 | bytes 3276804 | tf_op jit(solution)/shard_map/cond/branch_1_fun/dot_general | solution.py:175
  181.1 1.1 convert_element_type.139
  182.4 1.1 convert_element_type.140
  183.5 1.6 fusion.73
  185.1 2.3 %copy.92 = bf16[256,2048]{1,0:T(8,128)(2,1)} copy(bf16[256,2048]{1,0:T(8,128)(2,1)} %all-gather.4.cloned.1.call-done) | data formatting | bytes 2097152
  (104 shorter events, 34.2 us)
Async XLA Ops:
  7.2 132.3 %copy-start = (bf16[256,2048]{1,0:T(8,128)(2,1)S(1)}, bf16[256,2048]{1,0:T(8,128)(2,1)}, u32[]{:S(2)}) copy-start(bf16[256,2048]{1,0:T(8,128)(2,1)} %param.20) | copy-start | bytes 3145732
  7.2 64.4 %all-gather.6.cloned.1.call-start = ((), (), s32[]{:S(2)}) async-start(), calls=%async_computation.6 | async-start | bytes 2621440 | tf_op jit(solution)/shard_map/all_gather | solution.py:138
  9.5 8.8 %all-to-all-start = ((bf16[128,4,128]{2,0,1:T(8,128)(2,1)}), bf16[128,4,128]{2,0,1:T(8,128)(2,1)S(1)}, u32[]{:S(2)}, u32[]{:S(2)}) async-start(bf16[128,4,128]{2,0,1:T(8,128)(2,1)} %copy.44), calls=%async_computation | async-start | bytes 262144 | tf_op jit(solution)/shard_map/all_to_all | solution.py:36
  16.1 121.3 %copy-start.5 = (pred[512]{0:T(512)(128)(4,1)}, pred[512]{0:T(512)(128)(4,1)S(1)}, u32[]{:S(2)}) copy-start(pred[512]{0:T(512)(128)(4,1)S(1)} %get-tuple-element.955) | copy-start | bytes 1540
  18.4 12.6 %all-to-all-start.1 = ((bf16[128,4,256]{2,0,1:T(8,128)(2,1)}), bf16[128,4,256]{2,0,1:T(8,128)(2,1)S(1)}, u32[]{:S(2)}, u32[]{:S(2)}) async-start(bf16[128,4,256]{2,0,1:T(8,128)(2,1)} %copy.45), calls=%async_computation.1 | async-start | bytes 524288 | tf_op jit(solution)/shard_map/all_to_all | solution.py:35
  21.8 74.5 %reduce-scatter.2.cloned.1.call-start = ((), (), s32[]{:S(2)}) async-start(), calls=%async_computation.3 | async-start | bytes 1572864 | tf_op jit(solution)/shard_map/reduce_scatter | solution.py:155
  69.8 76.5 %copy-start.4 = (f32[2048]{0:T(1024)}, f32[2048]{0:T(1024)S(1)}, u32[]{:S(2)}) copy-start(f32[2048]{0:T(1024)S(1)} %get-tuple-element.1237) | copy-start | bytes 24580
  71.2 67.6 %copy-start.2 = (bf16[2048,64]{1,0:T(8,128)(2,1)}, bf16[2048,64]{1,0:T(8,128)(2,1)S(1)}, u32[]{:S(2)}) copy-start(bf16[2048,64]{1,0:T(8,128)(2,1)S(1)} %copy.46) | copy-start | bytes 786436
  74.9 62.5 %all-reduce.2.cloned.1.call-start = ((), (), s32[]{:S(2)}) async-start(), calls=%async_computation.4 | async-start | bytes 1048576 | tf_op jit(solution)/shard_map/psum | solution.py:158
  96.3 88.8 %all-gather.4.cloned.1.call-start = ((), (), s32[]{:S(2)}) async-start(), calls=%async_computation.5 | async-start | bytes 1572864 | tf_op jit(solution)/shard_map/all_gather | solution.py:159
  137.4 8.1 %copy-start.6 = (pred[512]{0:T(512)(128)(4,1)}, pred[512]{0:T(512)(128)(4,1)S(1)}, u32[]{:S(2)}) copy-start(pred[512]{0:T(512)(128)(4,1)S(1)} %get-tuple-element.971) | copy-start | bytes 1540
  139.5 6.9 %copy-start.1 = (bf16[2048,64]{1,0:T(8,128)(2,1)S(1)}, bf16[2048,64]{1,0:T(8,128)(2,1)}, u32[]{:S(2)}) copy-start(bf16[2048,64]{1,0:T(8,128)(2,1)} %get-tuple-element.1213) | copy-start | bytes 786436
  162.5 21.0 %collective-permute-start = (bf16[512,128]{1,0:T(8,128)(2,1)}, bf16[512,128]{1,0:T(8,128)(2,1)S(1)}, u32[]{:S(2)}, u32[]{:S(2)}) collective-permute-start(bf16[512,128]{1,0:T(8,128)(2,1)} %copy.49), channel_id=1, source_target_pairs={{0,4},{4,0},{1,5},{5,1},{2,6},{6,2},{3,7},{7,3},{8,12},{12,8},{9,1... | collective-permute-start | bytes 393224 | tf_op jit(solution)/shard_map/while/body/eval_jaxpr/ppermute | solution.py:12
  180.4 0.7 copy-start.3
Sparse Core Ops, SparseCore 0:
  9.5 28.0 all-gather.5
  75.0 21.2 reduce-scatter.1
  98.6 38.6 all-reduce.1
  138.7 21.0 all-gather.3
where the time goes:
time: 195 us; the launch traced here: 194 us
  waiting for transfers between devices  65.6 us (34%)
  local copies, waits for them, and re-layouts  42.3 us (22%)
  matrix products  29.5 us (15%)
  other arithmetic  22 us (11%)
  between operations  15.3 us (8%)
  starting transfers between devices  9.46 us (5%)
  blocking collectives  6.77 us (3%)
  loops' own time  3.02 us (2%)
    psum x1, waiting for transfers between devices, on_device(): shares = lax.psum(shares.astype(jnp.bfloat16), 'dp')  40.8 us
    reduce_scatter x1, waiting for transfers between devices, on_device(): lax.psum_scatter(weight_acc.astype(jnp.bfloat16), 'blk', scatter_dimensio...  21.4 us
    reshape x12, local copies, waits for them, and re-layouts, allowed_for(): expanded = jnp.broadcast_to(allowed[:, None, :], (local_rows, head_count,...  19 us
    dot_general x4, matrix products, score_block(): lax.dot_general(q_flat, key_block[:, :head_dim], (((1,), (1,)), ((), ()))...  6.93 us
    all_gather x1, blocking collectives, on_device(): shard_rows = lax.all_gather(kv_rows, 'blk', axis=0, tiled=True)  6.77 us
    broadcast_in_dim x6, local copies, waits for them, and re-layouts, allowed_for(): jnp.broadcast_to(allowed[:, None, :], (local_rows, head_count, span_rows))  6.66 us
    dot_general x2, matrix products, add_compute(): jnp.dot(probs.astype(jnp.bfloat16), key_block[:, head_dim:], preferred_el...  6.65 us
    dot_general x2, matrix products, contribute_compute(): jnp.dot(dscore, key_block[:, :head_dim], preferred_element_type=jnp.float32)  4.79 us
  transfers between devices with their start and end apart: 7, of which 4 were waited for; matrix products, arithmetic and copies ran while one was open for 44% of the time, Pallas kernels for 0%

commit v1 on v0

--- a/solution.py
+++ b/solution.py
@@ -1,6 +1,10 @@
+import functools
+
 import jax
 import jax.numpy as jnp
 from jax import lax
+from jax.experimental import pallas as pl
+from jax.experimental.pallas import tpu as pltpu
 from jax.sharding import PartitionSpec as P
 
 neg_fill = -1e30
@@ -219,9 +223,397 @@
     )
 
 
+MESH = pl.DeviceIdType.MESH
+f32, bf16 = jnp.float32, jnp.bfloat16
+NN = (((1,), (0,)), ((), ()))
+NT = (((1,), (1,)), ((), ()))
+
+
+def mm(a, b, dims=NN):
+    return lax.dot_general(a, b, dims, preferred_element_type=f32)
+
+
+def fused_kernel(
+    sizes,
+    q_ref,
+    kv_ref,
+    w_ref,
+    cot_ref,
+    len_ref,
+    flag_ref,
+    attn_ref,
+    gq_ref,
+    gkv_ref,
+    gw_ref,
+    qg,
+    kvl,
+    edge,
+    cotg,
+    qt,
+    ot,
+    dt32,
+    probs,
+    dkv,
+    back_out,
+    back_in,
+    wb,
+    r0,
+    r1,
+    r2,
+    qkv_send,
+    qkv_recv,
+    edge_send,
+    edge_recv,
+    cot_send,
+    cot_recv,
+    back_send,
+    back_recv,
+    red_send,
+    red_recv,
+):
+    rows, most, prefix, hd, heads, chunks, units = sizes
+    z, b, h = lax.axis_index("dp"), lax.axis_index("blk"), lax.axis_index("head")
+    block = 4 * rows
+    seq = 2 * block
+    hc = heads * hd
+    kvc = 2 * hd
+    span = rows + 2 * most
+    width = cot_ref.shape[1]
+    cw = width // chunks
+    uw = width // units
+    h1 = h + 1 - 2 * lax.rem(h, 2)
+    h2 = lax.rem(h + 2, 4)
+    h3 = 3 - h
+    peers = (h1, h2, h3)
+    za = z + 1 - 2 * lax.rem(z, 2)
+    zb = 3 - z
+    bit_a = lax.rem((z + 1) // 2, 2)
+    bit_b = z // 2
+    partners = (((za, b, h), bit_a), ((zb, b, h), bit_b), ((z, 1 - b, h), b))
+
+    barrier = pltpu.get_barrier_semaphore()
+    others = [(z, b, p) for p in peers] + [(z, 1 - b, p) for p in (h, h1, h2, h3)]
+    others += [(za, b, h), (zb, b, h)]
+    for who in others:
+        pl.semaphore_signal(barrier, inc=1, device_id=who, device_id_type=MESH)
+    pl.semaphore_wait(barrier, len(others))
+
+    def at(index, size):
+        return pl.ds(pl.multiple_of(index * size, size), size)
+
+    def remote(src, dst, send, recv, who):
+        return pltpu.make_async_remote_copy(
+            src_ref=src, dst_ref=dst, send_sem=send, recv_sem=recv,
+            device_id=who, device_id_type=MESH,
+        )
+
+    kv_rows = pl.ds(pl.multiple_of(most + h * rows, most), rows)
+    kv_copies, q_copies = [], []
+    for i, p in ((1, h2), (2, h3), (0, h1)):
+        kv_copies.append(remote(
+            kv_ref.at[:, at(p, kvc)], kvl.at[kv_rows],
+            qkv_send.at[i], qkv_recv.at[i], (z, b, p)))
+        q_copies.append(remote(
+            q_ref.at[:, at(p, hc)], qg.at[at(h, rows)],
+            qkv_send.at[3 + i], qkv_recv.at[3 + i], (z, b, p)))
+
+    def edge_copies(side):
+        first = 0 if side == 0 else rows - most
+        return [
+            remote(
+                kv_ref.at[pl.ds(first, most), at(p, kvc)], edge.at[side],
+                edge_send.at[j], edge_recv.at[side], (z, 1 - b, p))
+            for j, p in enumerate((h2, h3, h, h1))
+        ]
+
+    for c in kv_copies:
+        c.start()
+    for side, owner in ((0, 0), (1, 3)):
+        @pl.when(h == owner)
+        def _():
+            for c in edge_copies(side):
+                c.start()
+    for c in q_copies:
+        c.start()
+    cot_far, cot_near, cot_relay = [], [], []
+    for c in range(chunks):
+        piece = cot_ref.at[:, pl.ds(c * cw, cw)]
+        cot_far.append(remote(
+            piece, cotg.at[c, at(h, rows)], cot_send.at[c], cot_recv.at[c], (z, b, h2)))
+        cot_near.append(remote(
+            piece, cotg.at[c, at(h, rows)], cot_send.at[chunks + c],
+            cot_recv.at[chunks + c], (z, b, h1)))
+        cot_relay.append(remote(
+            cotg.at[c, at(h2, rows)], cotg.at[c, at(h2, rows)],
+            cot_send.at[2 * chunks + c], cot_recv.at[2 * chunks + c], (z, b, h1)))
+    for c in range(chunks):
+        cot_far[c].start()
+        cot_near[c].start()
+
+    qg[at(h, rows), :] = q_ref[:, at(h, hc)]
+    kvl[kv_rows, :] = kv_ref[:, at(h, kvc)]
+    for c in range(chunks):
+        cotg[c, at(h, rows), :] = cot_ref[:, c * cw : (c + 1) * cw]
+    dkv[...] = jnp.zeros_like(dkv)
+
+    lists = len_ref.shape[1]
+    len_row = len_ref[...].astype(f32)
+    flag_row = flag_ref[...].astype(f32)
+    ii = lax.broadcasted_iota(jnp.int32, (lists, lists), 0)
+    jj = lax.broadcasted_iota(jnp.int32, (lists, lists), 1)
+    len_col = jnp.sum(jnp.where(ii == jj, len_row, 0.0), axis=1, keepdims=True)
+    flag_col = jnp.sum(jnp.where(ii == jj, flag_row, 0.0), axis=1, keepdims=True)
+    start_col = prefix + jnp.sum(jnp.where(jj < ii, len_row, 0.0), axis=1, keepdims=True)
+    start_row = prefix + jnp.sum(jnp.where(ii < jj, len_col, 0.0), axis=0, keepdims=True)
+    base = (b * block).astype(f32)
+    key_total = block + 2 * most
+    kpos = lax.broadcasted_iota(jnp.int32, (key_total, 1), 0).astype(f32) + (base - most)
+    kseg = jnp.sum(jnp.where(start_row <= kpos, 1.0, 0.0), axis=1, keepdims=True)
+    kseg = jnp.where((kpos < prefix) | (kpos >= seq), -1.0, kseg)
+    ppos = lax.broadcasted_iota(jnp.int32, (prefix, 1), 0).astype(f32)
+    pseg = jnp.zeros((prefix, 1), f32)
+    qpos = lax.broadcasted_iota(jnp.int32, (1, block), 1).astype(f32) + base
+    qseg = jnp.sum(jnp.where(start_col <= qpos, 1.0, 0.0), axis=0, keepdims=True)
+    label = lax.broadcasted_iota(jnp.int32, (lists, 1), 0).astype(f32) + 1.0
+    qflag = jnp.sum(jnp.where(label == qseg, flag_col, 0.0), axis=0, keepdims=True)
+    qflag = qflag + jnp.where(qseg == 0.0, 1.0, 0.0)
+
+    for c in kv_copies:
+        c.wait_recv()
+    for side in range(2):
+        edge_copies(side)[0].wait_recv()
+    first = jnp.where(b == 0, kvl[most : most + prefix, :], edge[0, :prefix, :])
+    kvl[:most, :] = jnp.where(b == 0, jnp.zeros_like(edge[1]), edge[1])
+    kvl[most + block :, :] = jnp.where(b == 0, edge[0], jnp.zeros_like(edge[0]))
+    for c in q_copies:
+        c.wait_recv()
+    qt[...] = (qg[...].astype(f32) * (hd ** -0.5)).T.astype(bf16)
+    blank = jnp.zeros((hd, heads * rows), bf16)
+
+    def lanes(ref, tile):
+        return jnp.concatenate(
+            [ref[i * hd : (i + 1) * hd, tile * rows : (tile + 1) * rows] for i in range(heads)],
+            axis=1,
+        )
+
+    def stacked(value):
+        return jnp.concatenate(
+            [value[:, i * rows : (i + 1) * rows] for i in range(heads)], axis=0
+        )
+
+    def window(tile):
+        return jnp.concatenate([kvl[tile * rows : tile * rows + span, :], first], axis=0)
+
+    def forward(tile):
+        kw = window(tile)
+        scores = mm(kw, jnp.concatenate([lanes(qt, tile), blank], axis=0))
+        cut = slice(tile * rows, tile * rows + span)
+        kp = jnp.concatenate([kpos[cut], ppos], axis=0)
+        ks = jnp.concatenate([kseg[cut], pseg], axis=0)
+        sl = slice(tile * rows, (tile + 1) * rows)
+        qp, qs, qf = qpos[:, sl], qseg[:, sl], qflag[:, sl]
+        same = ks == qs
+        allowed = (same | (ks == 0.0)) & ((kp <= qp) | ((qf == 0.0) & same))
+        fill = jnp.where(allowed, 0.0, neg_fill)
+        scores = scores + jnp.concatenate([fill] * heads, axis=1)
+        best = jnp.max(scores, axis=0, keepdims=True)
+        e = jnp.exp(scores - best)
+        p = e * (1.0 / jnp.sum(e, axis=0, keepdims=True))
+        probs[tile] = p
+        out = stacked(mm(kw.T[hd:], p.astype(bf16)))
+        ot[:, sl] = out.astype(bf16)
+        attn_ref[sl, :] = out.T.astype(bf16)
+
+    def backward(tile):
+        kw = window(tile)
+        sl = slice(tile * rows, (tile + 1) * rows)
+        p = probs[tile]
+        d = lanes(dt32, tile).astype(bf16)
+        o = lanes(ot, tile)
+        row_dot = jnp.sum(d.astype(f32) * o.astype(f32), axis=0, keepdims=True)
+        d_pad = jnp.concatenate([blank, d], axis=0)
+        q_pad = jnp.concatenate([lanes(qt, tile), blank], axis=0)
+        ds = (p * (mm(kw, d_pad) - row_dot)).astype(bf16)
+        gq = stacked(mm(kw.T[:hd], ds)) * (hd ** -0.5)
+        gq_ref[sl, :] = gq.T.astype(bf16)
+        both = mm(ds, q_pad, NT) + mm(p.astype(bf16), d_pad, NT)
+        cut = slice(tile * rows, tile * rows + span)
+        dkv[cut, :] += both[:span]
+        tail = slice(key_total, key_total + prefix)
+        dkv[tail, :] += both[span:]
+
+    def reduce_copy(u, k):
+        dims = [partners[(u + i) % 3] for i in range(3)]
+        size = hc
+        keep = []
+        low = 0
+        for _, bit in dims:
+            size = size // 2
+            low = low + bit * size
+            keep.append((low, size))
+        sems = (red_send.at[u * 6 + k], red_recv.at[u * 6 + k])
+        if k < 3:
+            who, bit = dims[k]
+            low, size = keep[k]
+            away = low + (1 - 2 * bit) * size
+            src = wb.at[u, pl.ds(pl.multiple_of(away, size), size)]
+            return remote(src, (r0, r1, r2)[k].at[u], *sems, who)
+        low, size = keep[5 - k]
+        part = gw_ref.at[pl.ds(pl.multiple_of(low, size), size), pl.ds(u * uw, uw)]
+        return remote(part, part, *sems, dims[5 - k][0])
+
+    def reduce_step(u, k):
+        if k > 0:
+            reduce_copy(u, k - 1).wait_recv()
+        if 0 < k < 4:
+            dims = [partners[(u + i) % 3] for i in range(3)]
+            low, size = 0, hc
+            for _, bit in dims[:k]:
+                size = size // 2
+                low = low + bit * size
+            at_rows = pl.ds(pl.multiple_of(low, size), size)
+            total = wb[u, at_rows, :].astype(f32) + (r0, r1, r2)[k - 1][u].astype(f32)
+            if k < 3:
+                wb[u, at_rows, :] = total.astype(bf16)
+            else:
+                gw_ref[at_rows, u * uw : (u + 1) * uw] = total.astype(bf16)
+        if k < 6:
+            reduce_copy(u, k).start()
+
+    progress = [-1] * units
+
+    def advance(limit):
+        for u in range(limit):
+            if progress[u] < 6:
+                progress[u] += 1
+                reduce_step(u, progress[u])
+
+    per = units // chunks
+    for tile in range(4):
+        forward(tile)
+    for c in range(chunks):
+        cot_far[c].wait_recv()
+        cot_relay[c].start()
+        cot_near[c].wait_recv()
+        advance(c * per)
+        cot_relay[c].wait_recv()
+        whole = cotg[c]
+        grad = mm(ot[...], whole).astype(bf16)
+        for i in range(per):
+            wb[c * per + i] = grad[:, i * uw : (i + 1) * uw]
+        for i in range(per):
+            progress[c * per + i] = 0
+            reduce_step(c * per + i, 0)
+        part = mm(w_ref[:, c * cw : (c + 1) * cw], whole, NT)
+        if c == 0:
+            dt32[...] = part
+        else:
+            dt32[...] += part
+    for tile in range(4):
+        advance(units)
+        backward(tile)
+    zero_pre = jnp.zeros((most - prefix, kvc), f32)
+    pre = dkv[key_total : key_total + prefix, :]
+    pre_full = jnp.concatenate([pre, zero_pre], axis=0)
+    back_out[0] = jnp.where(b == 0, dkv[most + block : key_total, :], pre_full)
+    back_out[1] = dkv[:most, :]
+    backs = [
+        remote(back_out.at[i], back_in.at[i], back_send.at[i], back_recv.at[i], (z, 1 - b, h))
+        for i in range(2)
+    ]
+    for c in backs:
+        c.start()
+    advance(units)
+    for c in backs:
+        c.wait_recv()
+    head_part = dkv[most : 2 * most, :] + back_in[0] + jnp.where(b == 0, pre_full, 0.0)
+    gkv_ref[:most, :] = head_part.astype(bf16)
+    gkv_ref[most : block - most, :] = dkv[2 * most : block, :].astype(bf16)
+    gkv_ref[block - most :, :] = (dkv[block : block + most, :] + back_in[1]).astype(bf16)
+    while min(progress) < 6:
+        advance(units)
+    for c in kv_copies + q_copies + cot_far + cot_near + cot_relay + backs:
+        c.wait_send()
+    for side, owner in ((0, 0), (1, 3)):
+        @pl.when(h == owner)
+        def _():
+            for c in edge_copies(side):
+                c.wait_send()
+    for u in range(units):
+        for k in range(6):
+            reduce_copy(u, k).wait_send()
+
+
+def on_device_fused(queries, keys_values, out_weight, cotangent, passage_lengths, causal_flags):
+    chunks, units = 4, 8
+    rows = queries.shape[1]
+    block = 4 * rows
+    seq = 2 * block
+    most, prefix = seq // 16, seq // 32
+    kvc = keys_values.shape[2] // 4
+    hc = queries.shape[2] // 4
+    hd = kvc // 2
+    heads = hc // hd
+    width = cotangent.shape[2]
+    key_total = block + 2 * most
+    window = rows + 2 * most + prefix
+    vmem = pl.BlockSpec(memory_space=pltpu.VMEM)
+    uw = width // units
+    sem = pltpu.SemaphoreType.DMA
+    attn, gq, gkv, gw = pl.pallas_call(
+        functools.partial(fused_kernel, (rows, most, prefix, hd, heads, chunks, units)),
+        out_shape=(
+            jax.ShapeDtypeStruct((block, hc), bf16),
+            jax.ShapeDtypeStruct((block, hc), bf16),
+            jax.ShapeDtypeStruct((block, kvc), bf16),
+            jax.ShapeDtypeStruct((hc, width), bf16),
+        ),
+        in_specs=[vmem] * 6,
+        out_specs=(vmem,) * 4,
+        scratch_shapes=[
+            pltpu.VMEM((block, hc), bf16),
+            pltpu.VMEM((key_total, kvc), bf16),
+            pltpu.VMEM((2, most, kvc), bf16),
+            pltpu.VMEM((chunks, block, width // chunks), bf16),
+            pltpu.VMEM((hc, block), bf16),
+            pltpu.VMEM((hc, block), bf16),
+            pltpu.VMEM((hc, block), f32),
+            pltpu.VMEM((4, window, heads * rows), f32),
+            pltpu.VMEM((key_total + prefix, kvc), f32),
+            pltpu.VMEM((2, most, kvc), f32),
+            pltpu.VMEM((2, most, kvc), f32),
+            pltpu.VMEM((units, hc, uw), bf16),
+            pltpu.VMEM((units, hc // 2, uw), bf16),
+            pltpu.VMEM((units, hc // 4, uw), bf16),
+            pltpu.VMEM((units, hc // 8, uw), bf16),
+            sem((6,)),
+            sem((6,)),
+            sem((4,)),
+            sem((2,)),
+            sem((3 * chunks,)),
+            sem((3 * chunks,)),
+            sem((2,)),
+            sem((2,)),
+            sem((units * 6,)),
+            sem((units * 6,)),
+        ],
+        compiler_params=pltpu.CompilerParams(
+            collective_id=0, has_side_effects=True, vmem_limit_bytes=48 * 1024 * 1024
+        ),
+    )(
+        queries[0], keys_values[0], out_weight, cotangent[0], passage_lengths, causal_flags
+    )
+    return attn[None], gq[None], gkv[None], gw
+
+
+def fits(mesh):
+    sizes = (mesh.shape["dp"], mesh.shape["blk"], mesh.shape["head"])
+    return sizes == (4, 2, 4)
+
+
 def solution(mesh):
     return jax.shard_map(
-        on_device,
+        on_device_fused if fits(mesh) else on_device,
         mesh=mesh,
         in_specs=(
             P("dp", ("blk", "head"), None),

time: 195 us -> 69.4 us (0.36)
  waiting for transfers between devices: 65.6 us -> 0 us
  Pallas kernels: 0 us -> 60.7 us
  local copies, waits for them, and re-layouts: 42.3 us -> 7.81 us
  matrix products: 29.5 us -> 0 us
  other arithmetic: 22 us -> 0 us
  between operations: 15.3 us -> 0.66 us
  starting transfers between devices: 9.46 us -> 0 us
  blocking collectives: 6.77 us -> 0 us
  loops' own time: 3.02 us -> 0 us
    pallas_call x0 -> x1, Pallas kernels: none -> 60.7 us  [on_device_fused(): pl.pallas_call(functools.partial(fused_kernel, (rows, most, prefix, hd, h...]
    psum x1 -> x0, waiting for transfers between devices: 40.8 us -> none  [on_device(): shares = lax.psum(shares.astype(jnp.bfloat16), 'dp')]
    dot_general x16 -> x0, matrix products: 29.5 us -> none  [the longest x4 6.93 us: score_block(): lax.dot_general(q_flat, key_block[:, :head_dim], (((1,), (1,)), ((), ()))...]
    reshape x15 -> x0, local copies, waits for them, and re-layouts: 21.5 us -> none  [the longest x12 19 us: allowed_for(): expanded = jnp.broadcast_to(allowed[:, None, :], (local_rows, head_count,...]
    reduce_scatter x1 -> x0, waiting for transfers between devices: 21.4 us -> none  [on_device(): lax.psum_scatter(weight_acc.astype(jnp.bfloat16), 'blk', scatter_dimensio...]
    all_to_all x2 -> x0, starting transfers between devices: 7.65 us -> none  [the longest x1 4.24 us: on_device(): lax.all_to_all(keys_values[0], 'head', split_axis=1, concat_axis=0, tiled...]
    all_gather x1 -> x0, blocking collectives: 6.77 us -> none  [on_device(): shard_rows = lax.all_gather(kv_rows, 'blk', axis=0, tiled=True)]
    broadcast_in_dim x8 -> x0, local copies, waits for them, and re-layouts: 6.66 us -> none  [the longest x6 6.66 us: allowed_for(): jnp.broadcast_to(allowed[:, None, :], (local_rows, head_count, span_rows))]
  transfers between devices with their start and end apart: 7 -> 0, of which waited for: 4 -> 0; matrix products, arithmetic and copies ran while one was open for 44% -> 0% of each run, Pallas kernels for 0% -> 0%
where the time goes in v1:
time: 69.4 us; the launch traced here: 69.2 us
  Pallas kernels  60.7 us (87%)
  local copies, waits for them, and re-layouts  7.81 us (11%)
    pallas_call x1, Pallas kernels, on_device_fused(): pl.pallas_call(functools.partial(fused_kernel, (rows, most, prefix, hd, h...  60.7 us
    unnamed x16, local copies, waits for them, and re-layouts  7.81 us

profile of v1, /device:TPU:0, one launch (start us, length us, event | category | flops | bytes accessed | tf_op | source)
XLA Modules:
  0.0 69.2 jit_solution(11179937754234069157)
XLA Ops:
  0.6 0.0 copy-start.4
  0.6 0.0 copy-start.5
  0.7 0.6 copy-done.4
  1.3 0.0 copy-done.5
  1.3 0.0 copy-start
  1.3 1.2 %copy-done = bf16[256,2048]{1,0:T(8,128)(2,1)S(1)} copy-done((bf16[256,2048]{1,0:T(8,128)(2,1)S(1)}, bf16[256,2048]{1,0:T(8,128)(2,1)}, u32[]{:S(2)}) %copy-start) | copy-done | bytes 1048600
  2.5 0.0 copy-start.1
  2.5 1.0 %copy-done.1 = bf16[1,128,2048]{2,1,0:T(8,128)(2,1)S(1)} copy-done((bf16[1,128,2048]{2,1,0:T(8,128)(2,1)S(1)}, bf16[1,128,2048]{2,1,0:T(8,128)(2,1)}, u32[]{:S(2)}) %copy-start.1) | copy-done | bytes 524312
  3.6 0.0 copy-start.2
  3.6 0.9 %copy-done.2 = bf16[1,128,1024]{2,1,0:T(8,128)(2,1)S(1)} copy-done((bf16[1,128,1024]{2,1,0:T(8,128)(2,1)S(1)}, bf16[1,128,1024]{2,1,0:T(8,128)(2,1)}, u32[]{:S(2)}) %copy-start.2) | copy-done | bytes 262168
  4.5 0.0 copy-start.3
  4.5 0.9 %copy-done.3 = bf16[1,128,512]{2,1,0:T(8,128)(2,1)S(1)} copy-done((bf16[1,128,512]{2,1,0:T(8,128)(2,1)S(1)}, bf16[1,128,512]{2,1,0:T(8,128)(2,1)}, u32[]{:S(2)}) %copy-start.3) | copy-done | bytes 131096
  5.4 60.7 %shard_map.93 = (bf16[512,256]{1,0:T(8,128)(2,1)S(1)}, bf16[512,256]{1,0:T(8,128)(2,1)S(1)}, bf16[512,128]{1,0:T(8,128)(2,1)S(1)}, bf16[256,2048]{1,0:T(8,128)(2,1)S(1)}) custom-call(bf16[128,1024]{1,0:T(8,128)(2,1)S(1)} %bitcast.7, bf16[128,512]{1,0:T(8,128)(2,1)S(1)} %bitcast.10, bf16[256,2048]{1,0:T(8,128)(2,1)S(1)} %copy-done, ...), custom_call_target="tpu_custom_call" | custom-call | tf_op jit(solution)/shard_map/pallas_call | solution.py:563
  66.1 0.7 %copy.14 = bf16[1,512,256]{2,1,0:T(8,128)(2,1)} copy(bf16[1,512,256]{2,1,0:T(8,128)(2,1)S(1)} %bitcast.9) | data formatting | bytes 524288
  66.8 0.7 %copy.15 = bf16[1,512,256]{2,1,0:T(8,128)(2,1)} copy(bf16[1,512,256]{2,1,0:T(8,128)(2,1)S(1)} %bitcast.8) | data formatting | bytes 524288
  67.6 0.7 copy.16
  68.2 1.0 %copy.17 = bf16[256,2048]{1,0:T(8,128)(2,1)} copy(bf16[256,2048]{1,0:T(8,128)(2,1)S(1)} %get-tuple-element.19) | data formatting | bytes 2097152
Async XLA Ops:
  0.6 0.7 copy-start.4
  0.6 0.7 copy-start.5
  1.3 1.2 %copy-start = (bf16[256,2048]{1,0:T(8,128)(2,1)S(1)}, bf16[256,2048]{1,0:T(8,128)(2,1)}, u32[]{:S(2)}) copy-start(bf16[256,2048]{1,0:T(8,128)(2,1)} %w_ref.1) | copy-start | bytes 3145732
  2.5 1.0 %copy-start.1 = (bf16[1,128,2048]{2,1,0:T(8,128)(2,1)S(1)}, bf16[1,128,2048]{2,1,0:T(8,128)(2,1)}, u32[]{:S(2)}) copy-start(bf16[1,128,2048]{2,1,0:T(8,128)(2,1)} %param.9) | copy-start | bytes 1572868
  3.6 0.9 %copy-start.2 = (bf16[1,128,1024]{2,1,0:T(8,128)(2,1)S(1)}, bf16[1,128,1024]{2,1,0:T(8,128)(2,1)}, u32[]{:S(2)}) copy-start(bf16[1,128,1024]{2,1,0:T(8,128)(2,1)} %param.6) | copy-start | bytes 786436
  4.5 0.9 %copy-start.3 = (bf16[1,128,512]{2,1,0:T(8,128)(2,1)S(1)}, bf16[1,128,512]{2,1,0:T(8,128)(2,1)}, u32[]{:S(2)}) copy-start(bf16[1,128,512]{2,1,0:T(8,128)(2,1)} %param.7) | copy-start | bytes 393220

commit v2 on v1

--- a/solution.py
+++ b/solution.py
@@ -235,16 +235,20 @@
 
 def fused_kernel(
     sizes,
-    q_ref,
-    kv_ref,
-    w_ref,
-    cot_ref,
+    q_hbm,
+    kv_hbm,
+    w_hbm,
+    cot_hbm,
     len_ref,
     flag_ref,
     attn_ref,
     gq_ref,
     gkv_ref,
     gw_ref,
+    q_ref,
+    kv_ref,
+    w_ref,
+    local_sem,
     qg,
     kvl,
     edge,
@@ -278,7 +282,7 @@
     hc = heads * hd
     kvc = 2 * hd
     span = rows + 2 * most
-    width = cot_ref.shape[1]
+    width = cot_hbm.shape[1]
     cw = width // chunks
     uw = width // units
     h1 = h + 1 - 2 * lax.rem(h, 2)
@@ -286,8 +290,8 @@
     h3 = 3 - h
     peers = (h1, h2, h3)
     za = z + 1 - 2 * lax.rem(z, 2)
-    zb = 3 - z
-    bit_a = lax.rem((z + 1) // 2, 2)
+    zb = lax.rem(z + 2, 4)
+    bit_a = lax.rem(z, 2)
     bit_b = z // 2
     partners = (((za, b, h), bit_a), ((zb, b, h), bit_b), ((z, 1 - b, h), b))
 
@@ -296,7 +300,6 @@
     others += [(za, b, h), (zb, b, h)]
     for who in others:
         pl.semaphore_signal(barrier, inc=1, device_id=who, device_id_type=MESH)
-    pl.semaphore_wait(barrier, len(others))
 
     def at(index, size):
         return pl.ds(pl.multiple_of(index * size, size), size)
@@ -306,6 +309,18 @@
             src_ref=src, dst_ref=dst, send_sem=send, recv_sem=recv,
             device_id=who, device_id_type=MESH,
         )
+
+    loads = [
+        pltpu.make_async_copy(kv_hbm, kv_ref, local_sem.at[0]),
+        pltpu.make_async_copy(q_hbm, q_ref, local_sem.at[1]),
+    ]
+    for c in range(chunks):
+        loads.append(pltpu.make_async_copy(
+            cot_hbm.at[:, pl.ds(c * cw, cw)], cotg.at[c, at(h, rows)], local_sem.at[3 + c]))
+    loads.append(pltpu.make_async_copy(w_hbm, w_ref, local_sem.at[2]))
+    for c in loads:
+        c.start()
+    pl.semaphore_wait(barrier, len(others))
 
     kv_rows = pl.ds(pl.multiple_of(most + h * rows, most), rows)
     kv_copies, q_copies = [], []
@@ -326,6 +341,7 @@
             for j, p in enumerate((h2, h3, h, h1))
         ]
 
+    loads[0].wait()
     for c in kv_copies:
         c.start()
     for side, owner in ((0, 0), (1, 3)):
@@ -333,11 +349,12 @@
         def _():
             for c in edge_copies(side):
                 c.start()
+    loads[1].wait()
     for c in q_copies:
         c.start()
     cot_far, cot_near, cot_relay = [], [], []
     for c in range(chunks):
-        piece = cot_ref.at[:, pl.ds(c * cw, cw)]
+        piece = cotg.at[c, at(h, rows)]
         cot_far.append(remote(
             piece, cotg.at[c, at(h, rows)], cot_send.at[c], cot_recv.at[c], (z, b, h2)))
         cot_near.append(remote(
@@ -347,13 +364,12 @@
             cotg.at[c, at(h2, rows)], cotg.at[c, at(h2, rows)],
             cot_send.at[2 * chunks + c], cot_recv.at[2 * chunks + c], (z, b, h1)))
     for c in range(chunks):
+        loads[2 + c].wait()
         cot_far[c].start()
         cot_near[c].start()
 
     qg[at(h, rows), :] = q_ref[:, at(h, hc)]
     kvl[kv_rows, :] = kv_ref[:, at(h, kvc)]
-    for c in range(chunks):
-        cotg[c, at(h, rows), :] = cot_ref[:, c * cw : (c + 1) * cw]
     dkv[...] = jnp.zeros_like(dkv)
 
     lists = len_ref.shape[1]
@@ -442,8 +458,12 @@
         tail = slice(key_total, key_total + prefix)
         dkv[tail, :] += both[span:]
 
+    def order(u):
+        near, far, side = partners
+        return (near, side, far) if u % 3 == 1 else (side, near, far)
+
     def reduce_copy(u, k):
-        dims = [partners[(u + i) % 3] for i in range(3)]
+        dims = order(u)
         size = hc
         keep = []
         low = 0
@@ -466,7 +486,7 @@
         if k > 0:
             reduce_copy(u, k - 1).wait_recv()
         if 0 < k < 4:
-            dims = [partners[(u + i) % 3] for i in range(3)]
+            dims = order(u)
             low, size = 0, hc
             for _, bit in dims[:k]:
                 size = size // 2
@@ -482,20 +502,22 @@
 
     progress = [-1] * units
 
-    def advance(limit):
-        for u in range(limit):
-            if progress[u] < 6:
+    def advance(turn):
+        for u in range(units):
+            if 0 <= progress[u] < 6 and (turn - u) % 2 == 0:
                 progress[u] += 1
                 reduce_step(u, progress[u])
 
+    loads[2 + chunks].wait()
     per = units // chunks
     for tile in range(4):
-        forward(tile)
+        with jax.named_scope(f'fwd{tile}'):
+            forward(tile)
     for c in range(chunks):
         cot_far[c].wait_recv()
         cot_relay[c].start()
         cot_near[c].wait_recv()
-        advance(c * per)
+        advance(c)
         cot_relay[c].wait_recv()
         whole = cotg[c]
         grad = mm(ot[...], whole).astype(bf16)
@@ -510,8 +532,10 @@
         else:
             dt32[...] += part
     for tile in range(4):
-        advance(units)
-        backward(tile)
+        with jax.named_scope(f'adv{tile}'):
+            advance(units + tile)
+        with jax.named_scope(f'bwd{tile}'):
+            backward(tile)
     zero_pre = jnp.zeros((most - prefix, kvc), f32)
     pre = dkv[key_total : key_total + prefix, :]
     pre_full = jnp.concatenate([pre, zero_pre], axis=0)
@@ -523,15 +547,16 @@
     ]
     for c in backs:
         c.start()
-    advance(units)
+    turn = units + 4
+    while min(progress) < 6:
+        advance(turn)
+        turn += 1
     for c in backs:
         c.wait_recv()
     head_part = dkv[most : 2 * most, :] + back_in[0] + jnp.where(b == 0, pre_full, 0.0)
     gkv_ref[:most, :] = head_part.astype(bf16)
     gkv_ref[most : block - most, :] = dkv[2 * most : block, :].astype(bf16)
     gkv_ref[block - most :, :] = (dkv[block : block + most, :] + back_in[1]).astype(bf16)
-    while min(progress) < 6:
-        advance(units)
     for c in kv_copies + q_copies + cot_far + cot_near + cot_relay + backs:
         c.wait_send()
     for side, owner in ((0, 0), (1, 3)):
@@ -544,8 +569,32 @@
             reduce_copy(u, k).wait_send()
 
 
+def publish_kernel(*refs):
+    sems = refs[-1]
+    count = (len(refs) - 1) // 2
+    copies = [
+        pltpu.make_async_copy(refs[i], refs[count + i], sems.at[i]) for i in range(count)
+    ]
+    for c in copies:
+        c.start()
+    for c in copies:
+        c.wait()
+
+
+def publish(arrays):
+    done = pl.pallas_call(
+        publish_kernel,
+        out_shape=tuple(jax.ShapeDtypeStruct(a.shape, a.dtype) for a in arrays),
+        in_specs=[pl.BlockSpec(memory_space=pltpu.VMEM)] * len(arrays),
+        out_specs=(pl.BlockSpec(memory_space=pltpu.HBM),) * len(arrays),
+        scratch_shapes=[pltpu.SemaphoreType.DMA((len(arrays),))],
+        compiler_params=pltpu.CompilerParams(vmem_limit_bytes=8 * 1024 * 1024),
+    )(*arrays)
+    return tuple(a[None] for a in done[:-1]) + (done[-1],)
+
+
 def on_device_fused(queries, keys_values, out_weight, cotangent, passage_lengths, causal_flags):
-    chunks, units = 4, 8
+    chunks, units = 8, 8
     rows = queries.shape[1]
     block = 4 * rows
     seq = 2 * block
@@ -568,9 +617,13 @@
             jax.ShapeDtypeStruct((block, kvc), bf16),
             jax.ShapeDtypeStruct((hc, width), bf16),
         ),
-        in_specs=[vmem] * 6,
+        in_specs=[pl.BlockSpec(memory_space=pltpu.HBM)] * 4 + [vmem] * 2,
         out_specs=(vmem,) * 4,
         scratch_shapes=[
+            pltpu.VMEM(queries.shape[1:], bf16),
+            pltpu.VMEM(keys_values.shape[1:], bf16),
+            pltpu.VMEM(out_weight.shape, bf16),
+            sem((3 + chunks,)),
             pltpu.VMEM((block, hc), bf16),
             pltpu.VMEM((key_total, kvc), bf16),
             pltpu.VMEM((2, most, kvc), bf16),
@@ -598,12 +651,12 @@
             sem((units * 6,)),
         ],
         compiler_params=pltpu.CompilerParams(
-            collective_id=0, has_side_effects=True, vmem_limit_bytes=48 * 1024 * 1024
+            collective_id=0, has_side_effects=True, vmem_limit_bytes=51 * 1024 * 1024
         ),
     )(
         queries[0], keys_values[0], out_weight, cotangent[0], passage_lengths, causal_flags
     )
-    return attn[None], gq[None], gkv[None], gw
+    return publish((attn, gq, gkv, gw))
 
 
 def fits(mesh):

time: 69.4 us -> 57.8 us (0.83)
  Pallas kernels: 60.7 us -> 53.3 us
  local copies, waits for them, and re-layouts: 7.81 us -> 3.55 us
    pallas_call x1, Pallas kernels: 60.7 us -> 52.1 us  [on_device_fused(): pl.pallas_call(functools.partial(fused_kernel, (rows, most, prefix, hd, h...]
    unnamed x16 -> x10, local copies, waits for them, and re-layouts: 7.81 us -> 3.55 us
    pallas_call x0 -> x1, Pallas kernels: none -> 1.22 us  [publish(): pl.pallas_call(publish_kernel, out_shape=tuple((jax.ShapeDtypeStruct(a.sh...]
where the time goes in v2:
time: 57.8 us; the launch traced here: 57.5 us
  Pallas kernels  53.3 us (92%)
  local copies, waits for them, and re-layouts  3.55 us (6%)
  between operations  0.66 us (1%)
    pallas_call x1, Pallas kernels, on_device_fused(): pl.pallas_call(functools.partial(fused_kernel, (rows, most, prefix, hd, h...  52.1 us
    unnamed x10, local copies, waits for them, and re-layouts  3.55 us
    pallas_call x1, Pallas kernels, publish(): pl.pallas_call(publish_kernel, out_shape=tuple((jax.ShapeDtypeStruct(a.sh...  1.22 us

profile of v2, /device:TPU:0, one launch (start us, length us, event | category | flops | bytes accessed | tf_op | source)
XLA Modules:
  0.0 57.5 jit_solution(4376433294966844011)
XLA Ops:
  0.6 0.0 copy-start.3
  0.6 0.0 copy-start.4
  0.7 0.6 %copy-done.3 = s32[1,32]{1,0:T(1,128)S(1)} copy-done((s32[1,32]{1,0:T(1,128)S(1)}, s32[1,32]{1,0:T(1,128)}, u32[]{:S(2)}) %copy-start.3) | copy-done | bytes 152
  1.3 0.0 copy-done.4
  1.3 0.0 copy-start
  1.3 1.0 %copy-done = bf16[1,128,2048]{2,1,0:T(8,128)(2,1)S(1)} copy-done((bf16[1,128,2048]{2,1,0:T(8,128)(2,1)S(1)}, bf16[1,128,2048]{2,1,0:T(8,128)(2,1)}, u32[]{:S(2)}) %copy-start) | copy-done | bytes 524312
  2.3 0.0 copy-start.1
  2.3 0.9 %copy-done.1 = bf16[1,128,1024]{2,1,0:T(8,128)(2,1)S(1)} copy-done((bf16[1,128,1024]{2,1,0:T(8,128)(2,1)S(1)}, bf16[1,128,1024]{2,1,0:T(8,128)(2,1)}, u32[]{:S(2)}) %copy-start.1) | copy-done | bytes 262168
  3.3 0.0 copy-start.2
  3.3 0.9 %copy-done.2 = bf16[1,128,512]{2,1,0:T(8,128)(2,1)S(1)} copy-done((bf16[1,128,512]{2,1,0:T(8,128)(2,1)S(1)}, bf16[1,128,512]{2,1,0:T(8,128)(2,1)}, u32[]{:S(2)}) %copy-start.2) | copy-done | bytes 131096
  4.2 52.1 %shard_map.93 = (bf16[512,256]{1,0:T(8,128)(2,1)S(1)}, bf16[512,256]{1,0:T(8,128)(2,1)S(1)}, bf16[512,128]{1,0:T(8,128)(2,1)S(1)}, bf16[256,2048]{1,0:T(8,128)(2,1)S(1)}) custom-call(bf16[128,1024]{1,0:T(8,128)(2,1)S(1)} %bitcast.7, bf16[128,512]{1,0:T(8,128)(2,1)S(1)} %bitcast.8, bf16[256,2048]{1,0:T(8,128)(2,1)} %w_hbm.1, bf16[128,2048]{1,0:T(8,128)(2,1)S(1)} %bitcast.6, ...), custom_call_target="tpu_custom_call" | custom-call | tf_op jit(solution)/shard_map/pallas_call | solution.py:612
  56.3 1.2 %shard_map.94 = (bf16[512,256]{1,0:T(8,128)(2,1)}, bf16[512,256]{1,0:T(8,128)(2,1)}, bf16[512,128]{1,0:T(8,128)(2,1)}, bf16[256,2048]{1,0:T(8,128)(2,1)}) custom-call(bf16[512,256]{1,0:T(8,128)(2,1)S(1)} %get-tuple-element.12.refs_0_, bf16[512,256]{1,0:T(8,128)(2,1)S(1)} %get-tuple-element.13.refs_1_, bf16[512,128]{1,0:T(8,128)(2,1)S(1)} %get-tuple-element.14.refs_2_, ...), custom_call_target="tpu_custom_call" | custom-call | tf_op jit(solution)/shard_map/pallas_call | solution.py:585
Async XLA Ops:
  0.6 0.7 %copy-start.3 = (s32[1,32]{1,0:T(1,128)S(1)}, s32[1,32]{1,0:T(1,128)}, u32[]{:S(2)}) copy-start(s32[1,32]{1,0:T(1,128)} %len_ref.1) | copy-start | bytes 388
  0.6 0.7 %copy-start.4 = (s32[1,32]{1,0:T(1,128)S(1)}, s32[1,32]{1,0:T(1,128)}, u32[]{:S(2)}) copy-start(s32[1,32]{1,0:T(1,128)} %flag_ref.1) | copy-start | bytes 388
  1.3 1.0 %copy-start = (bf16[1,128,2048]{2,1,0:T(8,128)(2,1)S(1)}, bf16[1,128,2048]{2,1,0:T(8,128)(2,1)}, u32[]{:S(2)}) copy-start(bf16[1,128,2048]{2,1,0:T(8,128)(2,1)} %param.9) | copy-start | bytes 1572868
  2.3 0.9 %copy-start.1 = (bf16[1,128,1024]{2,1,0:T(8,128)(2,1)S(1)}, bf16[1,128,1024]{2,1,0:T(8,128)(2,1)}, u32[]{:S(2)}) copy-start(bf16[1,128,1024]{2,1,0:T(8,128)(2,1)} %param.6) | copy-start | bytes 786436
  3.3 0.9 %copy-start.2 = (bf16[1,128,512]{2,1,0:T(8,128)(2,1)S(1)}, bf16[1,128,512]{2,1,0:T(8,128)(2,1)}, u32[]{:S(2)}) copy-start(bf16[1,128,512]{2,1,0:T(8,128)(2,1)} %param.7) | copy-start | bytes 393220

commit v3 on v2

--- a/solution.py
+++ b/solution.py
@@ -503,8 +503,9 @@
     progress = [-1] * units
 
     def advance(turn):
-        for u in range(units):
-            if 0 <= progress[u] < 6 and (turn - u) % 2 == 0:
+        ranked = range(units) if turn < units else reversed(range(units))
+        for u in ranked:
+            if 0 <= progress[u] < 5 and turn - u >= 3 and (turn - u) % 2 == 1:
                 progress[u] += 1
                 reduce_step(u, progress[u])
 
@@ -548,9 +549,11 @@
     for c in backs:
         c.start()
     turn = units + 4
-    while min(progress) < 6:
+    while min(progress) < 5:
         advance(turn)
         turn += 1
+    for u in range(units):
+        reduce_step(u, 6)
     for c in backs:
         c.wait_recv()
     head_part = dkv[most : 2 * most, :] + back_in[0] + jnp.where(b == 0, pre_full, 0.0)

time: 57.8 us -> 53.9 us (0.933)
  Pallas kernels: 53.3 us -> 49.5 us
    pallas_call x1, Pallas kernels: 52.1 us -> 48.2 us  [on_device_fused(): pl.pallas_call(functools.partial(fused_kernel, (rows, most, prefix, hd, h...]
where the time goes in v3:
time: 53.9 us; the launch traced here: 53.7 us
  Pallas kernels  49.5 us (92%)
  local copies, waits for them, and re-layouts  3.55 us (7%)
  between operations  0.66 us (1%)
    pallas_call x1, Pallas kernels, on_device_fused(): pl.pallas_call(functools.partial(fused_kernel, (rows, most, prefix, hd, h...  48.2 us
    unnamed x10, local copies, waits for them, and re-layouts  3.55 us
    pallas_call x1, Pallas kernels, publish(): pl.pallas_call(publish_kernel, out_shape=tuple((jax.ShapeDtypeStruct(a.sh...  1.22 us

profile of v3, /device:TPU:0, one launch (start us, length us, event | category | flops | bytes accessed | tf_op | source)
XLA Modules:
  0.0 53.7 jit_solution(17334651398606533291)
XLA Ops:
  0.6 0.0 copy-start.3
  0.6 0.0 copy-start.4
  0.7 0.6 %copy-done.3 = s32[1,32]{1,0:T(1,128)S(1)} copy-done((s32[1,32]{1,0:T(1,128)S(1)}, s32[1,32]{1,0:T(1,128)}, u32[]{:S(2)}) %copy-start.3) | copy-done | bytes 152
  1.3 0.0 copy-done.4
  1.3 0.0 copy-start
  1.3 1.0 %copy-done = bf16[1,128,2048]{2,1,0:T(8,128)(2,1)S(1)} copy-done((bf16[1,128,2048]{2,1,0:T(8,128)(2,1)S(1)}, bf16[1,128,2048]{2,1,0:T(8,128)(2,1)}, u32[]{:S(2)}) %copy-start) | copy-done | bytes 524312
  2.3 0.0 copy-start.1
  2.3 0.9 %copy-done.1 = bf16[1,128,1024]{2,1,0:T(8,128)(2,1)S(1)} copy-done((bf16[1,128,1024]{2,1,0:T(8,128)(2,1)S(1)}, bf16[1,128,1024]{2,1,0:T(8,128)(2,1)}, u32[]{:S(2)}) %copy-start.1) | copy-done | bytes 262168
  3.3 0.0 copy-start.2
  3.3 0.9 %copy-done.2 = bf16[1,128,512]{2,1,0:T(8,128)(2,1)S(1)} copy-done((bf16[1,128,512]{2,1,0:T(8,128)(2,1)S(1)}, bf16[1,128,512]{2,1,0:T(8,128)(2,1)}, u32[]{:S(2)}) %copy-start.2) | copy-done | bytes 131096
  4.2 48.2 %shard_map.93 = (bf16[512,256]{1,0:T(8,128)(2,1)S(1)}, bf16[512,256]{1,0:T(8,128)(2,1)S(1)}, bf16[512,128]{1,0:T(8,128)(2,1)S(1)}, bf16[256,2048]{1,0:T(8,128)(2,1)S(1)}) custom-call(bf16[128,1024]{1,0:T(8,128)(2,1)S(1)} %bitcast.7, bf16[128,512]{1,0:T(8,128)(2,1)S(1)} %bitcast.8, bf16[256,2048]{1,0:T(8,128)(2,1)} %w_hbm.1, bf16[128,2048]{1,0:T(8,128)(2,1)S(1)} %bitcast.6, ...), custom_call_target="tpu_custom_call" | custom-call | tf_op jit(solution)/shard_map/pallas_call | solution.py:615
  52.4 1.2 %shard_map.94 = (bf16[512,256]{1,0:T(8,128)(2,1)}, bf16[512,256]{1,0:T(8,128)(2,1)}, bf16[512,128]{1,0:T(8,128)(2,1)}, bf16[256,2048]{1,0:T(8,128)(2,1)}) custom-call(bf16[512,256]{1,0:T(8,128)(2,1)S(1)} %get-tuple-element.12.refs_0_, bf16[512,256]{1,0:T(8,128)(2,1)S(1)} %get-tuple-element.13.refs_1_, bf16[512,128]{1,0:T(8,128)(2,1)S(1)} %get-tuple-element.14.refs_2_, ...), custom_call_target="tpu_custom_call" | custom-call | tf_op jit(solution)/shard_map/pallas_call | solution.py:588
Async XLA Ops:
  0.6 0.7 %copy-start.3 = (s32[1,32]{1,0:T(1,128)S(1)}, s32[1,32]{1,0:T(1,128)}, u32[]{:S(2)}) copy-start(s32[1,32]{1,0:T(1,128)} %len_ref.1) | copy-start | bytes 388
  0.6 0.7 %copy-start.4 = (s32[1,32]{1,0:T(1,128)S(1)}, s32[1,32]{1,0:T(1,128)}, u32[]{:S(2)}) copy-start(s32[1,32]{1,0:T(1,128)} %flag_ref.1) | copy-start | bytes 388
  1.3 1.0 %copy-start = (bf16[1,128,2048]{2,1,0:T(8,128)(2,1)S(1)}, bf16[1,128,2048]{2,1,0:T(8,128)(2,1)}, u32[]{:S(2)}) copy-start(bf16[1,128,2048]{2,1,0:T(8,128)(2,1)} %param.9) | copy-start | bytes 1572868
  2.3 0.9 %copy-start.1 = (bf16[1,128,1024]{2,1,0:T(8,128)(2,1)S(1)}, bf16[1,128,1024]{2,1,0:T(8,128)(2,1)}, u32[]{:S(2)}) copy-start(bf16[1,128,1024]{2,1,0:T(8,128)(2,1)} %param.6) | copy-start | bytes 786436
  3.3 0.9 %copy-start.2 = (bf16[1,128,512]{2,1,0:T(8,128)(2,1)S(1)}, bf16[1,128,512]{2,1,0:T(8,128)(2,1)}, u32[]{:S(2)}) copy-start(bf16[1,128,512]{2,1,0:T(8,128)(2,1)} %param.7) | copy-start | bytes 393220
